TPU v7x, 32 devices: a whole 2x2x4 slice. The times are simulated.
32 devices in a mesh: blk: 8 (over z, x), order: 4 (over y, core).
Axes of the slice: x: 2, y: 2, z: 4, core: 2. Of those that a mesh axis runs over, the one named last changes fastest.
Arguments:
- field: float32 [16, 512, 4096], P(None, 'blk', 'order'), may hold values from -6 to 6
- ocean_mask: int32 [512, 4096], P('blk', 'order'), may hold values from 0 to 1, as said below
- plan: int32 [512], replicated, may hold values from 0 to 384, as said below
- legendre: bfloat16 [384, 1024, 1024], P('blk', 'order'), may hold values from -0.4375 to 0.4375
Outputs:
- coefficients: float32 [1024, 16, 2, 1024], P('blk', None, None, 'order')
Inputs may be any that keep to these rules, and one draw needn't show every extreme that they name: `ocean_mask`: exactly 128 cycles are all land, at the ends of the cycle order; every other cycle has an ocean point. plan is 384 exactly at the cycles that are all land, and names every slot below 384 once at the other cycles; slot p belongs to index p // 48 of blk; the cycles of one index of blk name at most 8 slots of one index, and in every draw some index of blk names exactly 8 slots of some index.
All inputs are finite; a program needn't handle non-finite values.
Results may differ from a plain program's by a relative error of at most 0.0029.
Values may be sent and summed in bfloat16 or wider, within the bound.
A program may use at most 128 MiB of HBM per device.

v0:
```python
import math

import jax
import jax.numpy as jnp
from jax import lax
from jax.sharding import PartitionSpec as P

NLON = 4096
M = 1024


def twiddle(first, count):
    longitudes = first + jnp.arange(count, dtype=jnp.int32)
    orders = jnp.arange(M, dtype=jnp.int32)
    product = longitudes[:, None] * orders[None, :] % NLON
    angle = product.astype(jnp.float32) * (2.0 * math.pi / NLON)
    scale = 1.0 / math.sqrt(NLON)
    return jnp.stack([jnp.cos(angle) * scale, -jnp.sin(angle) * scale], axis=1)


def transform(values, table):
    return jnp.einsum("frn,ncm->frcm", values, table, precision=lax.Precision.HIGHEST)


def pack_cycles(masked, plan, slot_dev):
    n_blk = lax.axis_size("blk")
    own_index = lax.axis_index("blk")
    cycle_dev = masked.shape[1]
    cap = (cycle_dev + n_blk - 1) // n_blk
    grid = plan.reshape(n_blk, cycle_dev)
    owner = grid // slot_dev
    positions = jnp.arange(cycle_dev, dtype=jnp.int32)
    earlier = positions[None, :] < positions[:, None]
    same_owner = owner[:, :, None] == owner[:, None, :]
    rank = jnp.sum(same_owner & earlier[None], axis=2, dtype=jnp.int32)
    send_pos = owner * cap + rank
    local_pos = lax.dynamic_index_in_dim(send_pos, own_index, 0, keepdims=False)
    buffer_ids = jnp.arange(n_blk * cap, dtype=jnp.int32)
    send_onehot = (buffer_ids[:, None] == local_pos[None, :]).astype(jnp.float32)
    outgoing = jnp.einsum("qr,frn->fqn", send_onehot, masked, precision=lax.Precision.HIGHEST)
    arrived = lax.all_to_all(outgoing, "blk", split_axis=1, concat_axis=1, tiled=True)
    source_pos = (jnp.arange(n_blk, dtype=jnp.int32)[:, None] * cap + rank).reshape(-1)
    mine = (owner == own_index).reshape(-1)
    slot_local = (grid % slot_dev).reshape(-1)
    slot_ids = jnp.arange(slot_dev, dtype=jnp.int32)
    slot_onehot = ((slot_local[None, :] == slot_ids[:, None]) & mine[None, :]).astype(jnp.float32)
    source_onehot = (source_pos[:, None] == buffer_ids[None, :]).astype(jnp.float32)
    receive_map = jnp.dot(slot_onehot, source_onehot, precision=lax.Precision.HIGHEST)
    return jnp.einsum("pq,fqn->fpn", receive_map, arrived, precision=lax.Precision.HIGHEST)


def body(field, ocean_mask, plan, legendre):
    lon_local = field.shape[2]
    slot_dev = legendre.shape[0]
    masked = field * ocean_mask.astype(jnp.float32)[None]
    packed = pack_cycles(masked, plan, slot_dev)
    first = lax.axis_index("order") * lon_local
    terms = transform(packed, twiddle(first, lon_local))
    spectrum = lax.psum_scatter(terms, "order", scatter_dimension=3, tiled=True).astype(
        jnp.bfloat16
    )
    terms = jnp.einsum("pml,fpcm->lfcm", legendre, spectrum, preferred_element_type=jnp.float32)
    coefficients = lax.psum_scatter(terms, "blk", scatter_dimension=0, tiled=True)
    return coefficients


def solution(mesh):
    placed = (P(None, "blk", "order"), P("blk", "order"), P(), P("blk", "order", None))
    return jax.shard_map(
        body, mesh=mesh, in_specs=placed, out_specs=P("blk", None, None, "order"), check_vma=False
    )
```

profile of v0, /device:TPU:0, one launch (start us, length us, event | category | flops | bytes accessed | tf_op | source)
XLA Modules:
  0.0 815.6 jit_solution(1129262318180836919)
XLA Ops:
  6.6 0.7 fusion.31
  7.3 0.1 and.67
  7.3 0.1 div.20
  7.4 1.0 convert_element_type.26
  8.4 0.3 convert_reduce_fusion
  8.7 0.1 multiply_add_fusion
  8.8 5.5 fusion.19
  14.3 4.5 copy.9
  18.8 0.0 copy-start.1
  18.8 7.4 all-to-all-start
  26.2 0.0 reduce-scatter.3.cloned.1.call-start
  26.3 0.1 add.77
  26.4 0.0 copy-done.1
  26.4 0.3 convolution_bitcast_fusion
  26.6 19.0 %cosine_multiply_fusion = (f32[1024,1,1024]{2,0,1:T(8,128)}, f32[1024,1,1024]{2,0,1:T(8,128)}) fusion(s32[1024]{0:T(1024)S(1)} %iota_add_fusion), kind=kLoop, calls=%fused_computation.16 | loop fusion | flops 17825792 | bytes 8392704 | tf_op jit(solution)/shard_map/mul | solution.py:18
  45.7 73.8 %all-to-all-done = f32[16,64,1024]{2,0,1:T(8,128)} async-done(((f32[16,64,1024]{2,0,1:T(8,128)}), f32[16,64,1024]{2,0,1:T(8,128)}, u32[]{:S(2)}, u32[]{:S(2)}) %all-to-all-start) | async-done | bytes 4194336 | tf_op jit(solution)/shard_map/all_to_all | solution.py:41
  119.5 0.0 copy-start
  119.5 8.1 fusion.11
  127.7 0.0 copy-done
  127.7 23.8 %fusion.5 = f32[16,48,2,1024]{3,1,2,0:T(8,128)} fusion(f32[1024,1,1024]{2,0,1:T(8,128)} %get-tuple-element.11, f32[1024,1,1024]{2,0,1:T(8,128)S(1)} %copy-done, f32[16,1024,48]{1,2,0:T(8,128)S(1)} %fusion.11), kind=kOutput, calls=%fused_computation.4 | convolution fusion | flops 19329449984 | bytes 17825792 | tf_op jit(solution)/shard_map/frn,ncm->frcm/dot_general | solution.py:22
  151.5 0.0 reduce-scatter.3.cloned.1.call-update
  151.5 0.0 reduce-scatter.5.cloned.1.call-start
  151.6 57.1 %reduce-scatter.3.cloned.1.call-done = f32[16,48,2,256]{3,1,2,0:T(8,128)} async-done(((f32[16,48,2,1024]{3,1,2,0:T(8,128)}), f32[16,48,2,256]{3,1,2,0:T(8,128)}) %reduce-scatter.3.cloned.1.call-update) | async-done | bytes 1572880 | tf_op jit(solution)/shard_map/reduce_scatter | solution.py:59
  208.7 1.5 convert_element_type.29
  210.2 3.0 copy.11
  213.2 51.2 %fusion.2 = f32[1024,16,2,256]{0,1,2,3:T(8,128)} fusion(bf16[16,48,2,256]{1,0,2,3:T(8,128)(2,1)S(1)} %copy.11, bf16[48,256,1024,1]{2,1,0,3:T(8,128)(2,1)} %bitcast.24), kind=kOutput, calls=%fused_computation.2 | convolution fusion | flops 805306368 | bytes 59506688 | tf_op jit(solution)/shard_map/pml,fpcm->lfcm/dot_general | solution.py:62
  264.4 0.0 reduce-scatter.5.cloned.1.call-update
  264.4 538.6 %reduce-scatter.5.cloned.1.call-done = f32[128,16,2,256]{0,1,2,3:T(8,128)} async-done(((f32[1024,16,2,256]{0,1,2,3:T(8,128)}), f32[128,16,2,256]{0,1,2,3:T(8,128)}) %reduce-scatter.5.cloned.1.call-update) | async-done | bytes 4194320 | tf_op jit(solution)/shard_map/reduce_scatter | solution.py:63
  803.0 5.8 copy.13
  (6 shorter events, 0.0 us)
Async XLA Ops:
  18.8 7.6 copy-start.1
  18.8 100.7 %all-to-all-start = ((f32[16,64,1024]{2,0,1:T(8,128)}), f32[16,64,1024]{2,0,1:T(8,128)}, u32[]{:S(2)}, u32[]{:S(2)}) async-start(f32[16,64,1024]{2,0,1:T(8,128)} %copy.9), calls=%async_computation | async-start | bytes 8388608 | tf_op jit(solution)/shard_map/all_to_all | solution.py:41
  26.2 182.4 %reduce-scatter.3.cloned.1.call-start = ((), (), s32[]{:S(2)}) async-start(), calls=%async_computation.3 | async-start | bytes 7864320 | tf_op jit(solution)/shard_map/reduce_scatter | solution.py:59
  119.5 8.2 copy-start
  151.5 651.5 %reduce-scatter.5.cloned.1.call-start = ((), (), s32[]{:S(2)}) async-start(), calls=%async_computation.4 | async-start | bytes 37748736 | tf_op jit(solution)/shard_map/reduce_scatter | solution.py:63
Sparse Core Ops, SparseCore 0:
  151.7 56.9 reduce-scatter.2
  264.5 538.4 reduce-scatter.4
where the time goes:
time: 816 us
  waiting for transfers between devices  670 us (82%)
  matrix products  88.9 us (11%)
  other arithmetic  22.6 us (3%)
  local copies, waits for them, and re-layouts  13.6 us (2%)
  between operations  13.5 us (2%)
    reduce_scatter x1, waiting for transfers between devices, body(): lax.psum_scatter(terms, 'blk', scatter_dimension=0, tiled=True)  539 us
    all_to_all x1, waiting for transfers between devices, pack_cycles(): lax.all_to_all(outgoing, 'blk', split_axis=1, concat_axis=1, tiled=True)  73.8 us
    reduce_scatter x1, waiting for transfers between devices, body(): lax.psum_scatter(terms, 'order', scatter_dimension=3, tiled=True)  57.1 us
    dot_general x1, matrix products, body(): jnp.einsum('pml,fpcm->lfcm', legendre, spectrum, preferred_element_type=j...  51.2 us
    dot_general x1, matrix products, transform(): jnp.einsum('frn,ncm->frcm', values, table, precision=lax.Precision.HIGHEST)  23.8 us
    mul x1, other arithmetic, twiddle(): return jnp.stack([jnp.cos(angle) * scale, -jnp.sin(angle) * scale], axis=1)  19 us
  transfers between devices with their start and end apart: 3, of which 3 were waited for; matrix products, arithmetic and copies ran while one was open for 2% of the time, Pallas kernels for 0%

commit v1 on v0

--- a/solution.py
+++ b/solution.py
@@ -49,6 +49,35 @@
     return jnp.einsum("pq,fqn->fpn", receive_map, arrived, precision=lax.Precision.HIGHEST)
 
 
+def degree_sums(legendre, spectrum):
+    n_blk = lax.axis_size("blk")
+    own_index = lax.axis_index("blk")
+    pairs = n_blk // 2
+    degree_dev = legendre.shape[2] // n_blk
+    own_pair, own_side = own_index // 2, own_index % 2
+    swap = [(i, i + 1 - 2 * (i % 2)) for i in range(n_blk)]
+
+    def terms_for(target):
+        table = lax.dynamic_slice_in_dim(legendre, target * degree_dev, degree_dev, 2)
+        return jnp.einsum("pml,fpcm->lfcm", table, spectrum, preferred_element_type=jnp.float32)
+
+    def pair_sum(step):
+        base = (own_pair + step) % pairs * 2
+        given = terms_for(base + 1 - own_side).astype(jnp.bfloat16)
+        taken = lax.ppermute(given, "blk", swap)
+        return terms_for(base + own_side) + taken.astype(jnp.float32)
+
+    steps = sorted(range(1, pairs), key=lambda step: abs(2 * step - pairs))
+    arrived = []
+    for step in steps:
+        shift = [(i, (i + 2 * step) % n_blk) for i in range(n_blk)]
+        arrived.append(lax.ppermute(pair_sum(step).astype(jnp.bfloat16), "blk", shift))
+    total = pair_sum(0)
+    for piece in arrived:
+        total = total + piece.astype(jnp.float32)
+    return total
+
+
 def body(field, ocean_mask, plan, legendre):
     lon_local = field.shape[2]
     slot_dev = legendre.shape[0]
@@ -59,8 +88,7 @@
     spectrum = lax.psum_scatter(terms, "order", scatter_dimension=3, tiled=True).astype(
         jnp.bfloat16
     )
-    terms = jnp.einsum("pml,fpcm->lfcm", legendre, spectrum, preferred_element_type=jnp.float32)
-    coefficients = lax.psum_scatter(terms, "blk", scatter_dimension=0, tiled=True)
+    coefficients = degree_sums(legendre, spectrum)
     return coefficients
 
 

time: 816 us -> 474 us (0.58)
  waiting for transfers between devices: 670 us -> 316 us
  matrix products: 88.9 us -> 57.3 us
  local copies, waits for them, and re-layouts: 13.6 us -> 32.9 us
  starting transfers between devices: 7.5 us -> 19.4 us
    reduce_scatter x1 -> x0, waiting for transfers between devices: 539 us -> none  [body(): lax.psum_scatter(terms, 'blk', scatter_dimension=0, tiled=True)]
    ppermute x0 -> x7, waiting for transfers between devices: none -> 205 us  [the longest x4 155 us: pair_sum(): taken = lax.ppermute(given, 'blk', swap)]
    dot_general x1 -> x8, matrix products: 51.2 us -> 19.6 us  [terms_for(): jnp.einsum('pml,fpcm->lfcm', table, spectrum, preferred_element_type=jnp....]
    reduce_scatter x1, waiting for transfers between devices: 57.1 us -> 37.9 us  [body(): lax.psum_scatter(terms, 'order', scatter_dimension=3, tiled=True)]
    dynamic_slice x0 -> x1, local copies, waits for them, and re-layouts: none -> 19.1 us  [terms_for(): lax.dynamic_slice_in_dim(legendre, target * degree_dev, degree_dev, 2)]
    ppermute x0 -> x7, starting transfers between devices: none -> 11.9 us  [the longest x3 7.6 us: degree_sums(): lax.ppermute(pair_sum(step).astype(jnp.bfloat16), 'blk', shift)]
  transfers between devices with their start and end apart: 3 -> 9, of which waited for: 3 -> 7; matrix products, arithmetic and copies ran while one was open for 2% -> 12% of each run, Pallas kernels for 0% -> 0%
where the time goes in v1:
time: 474 us; the launch traced here: 466 us
  waiting for transfers between devices  316 us (67%)
  matrix products  57.3 us (12%)
  local copies, waits for them, and re-layouts  32.9 us (7%)
  other arithmetic  26 us (5%)
  starting transfers between devices  19.4 us (4%)
  between operations  14.1 us (3%)
    ppermute x4, waiting for transfers between devices, pair_sum(): taken = lax.ppermute(given, 'blk', swap)  155 us
    all_to_all x1, waiting for transfers between devices, pack_cycles(): lax.all_to_all(outgoing, 'blk', split_axis=1, concat_axis=1, tiled=True)  73.8 us
    ppermute x3, waiting for transfers between devices, degree_sums(): lax.ppermute(pair_sum(step).astype(jnp.bfloat16), 'blk', shift)  50.1 us
    reduce_scatter x1, waiting for transfers between devices, body(): lax.psum_scatter(terms, 'order', scatter_dimension=3, tiled=True)  37.9 us
    dot_general x1, matrix products, transform(): jnp.einsum('frn,ncm->frcm', values, table, precision=lax.Precision.HIGHEST)  23.8 us
    dot_general x8, matrix products, terms_for(): jnp.einsum('pml,fpcm->lfcm', table, spectrum, preferred_element_type=jnp....  19.6 us
    dynamic_slice x1, local copies, waits for them, and re-layouts, terms_for(): lax.dynamic_slice_in_dim(legendre, target * degree_dev, degree_dev, 2)  19.1 us
    mul x1, other arithmetic, twiddle(): return jnp.stack([jnp.cos(angle) * scale, -jnp.sin(angle) * scale], axis=1)  19 us
  transfers between devices with their start and end apart: 9, of which 7 were waited for; matrix products, arithmetic and copies ran while one was open for 12% of the time, Pallas kernels for 0%

profile of v1, /device:TPU:0, one launch (start us, length us, event | category | flops | bytes accessed | tf_op | source)
XLA Modules:
  0.0 466.1 jit_solution(10730977180983548286)
XLA Ops:
  7.4 1.0 convert_element_type.80
  8.8 5.5 %fusion.28 = f32[16,64,1024]{2,1,0:T(8,128)S(1)} fusion(f32[16,64,1024]{2,1,0:T(8,128)} %param.4, f32[64,1024]{1,0:T(8,128)S(1)} %convert_element_type.80, s32[64]{0:T(128)S(1)} %fusion.42), kind=kOutput, calls=%fused_computation.46 | convolution fusion | flops 806359040 | bytes 8651008 | tf_op jit(solution)/shard_map/qr,frn->fqn/dot_general | solution.py:40
  14.3 4.5 copy.39
  18.8 7.4 %all-to-all-start = ((f32[16,64,1024]{2,0,1:T(8,128)}), f32[16,64,1024]{2,0,1:T(8,128)}, u32[]{:S(2)}, u32[]{:S(2)}) async-start(f32[16,64,1024]{2,0,1:T(8,128)} %copy.39), calls=%async_computation | async-start | bytes 8388608 | tf_op jit(solution)/shard_map/all_to_all | solution.py:41
  26.6 19.0 %cosine_multiply_fusion = (f32[1024,1,1024]{2,0,1:T(8,128)}, f32[1024,1,1024]{2,0,1:T(8,128)}) fusion(s32[1024]{0:T(1024)S(1)} %iota_add_fusion), kind=kLoop, calls=%fused_computation.23 | loop fusion | flops 17825792 | bytes 8392704 | tf_op jit(solution)/shard_map/mul | solution.py:18
  45.7 73.8 %all-to-all-done = f32[16,64,1024]{2,0,1:T(8,128)} async-done(((f32[16,64,1024]{2,0,1:T(8,128)}), f32[16,64,1024]{2,0,1:T(8,128)}, u32[]{:S(2)}, u32[]{:S(2)}) %all-to-all-start) | async-done | bytes 4194336 | tf_op jit(solution)/shard_map/all_to_all | solution.py:41
  119.5 8.1 %fusion.12 = f32[16,1024,48]{1,2,0:T(8,128)S(1)} fusion(f32[48,64,1]{1,0,2:T(8,128)S(1)} %convolution_bitcast_fusion, f32[16,64,1024]{2,0,1:T(8,128)} %all-to-all-done), kind=kOutput, calls=%fused_computation.20 | convolution fusion | flops 603979776 | bytes 7352320 | tf_op jit(solution)/shard_map/pq,fqn->fpn/dot_general | solution.py:49
  127.7 23.8 %fusion = f32[16,48,2,1024]{3,1,2,0:T(8,128)} fusion(f32[1024,1,1024]{2,0,1:T(8,128)} %get-tuple-element.19, f32[1024,1,1024]{2,0,1:T(8,128)S(1)} %copy-done.7, f32[16,1024,48]{1,2,0:T(8,128)S(1)} %fusion.12), kind=kOutput, calls=%fused_computation.1 | convolution fusion | flops 19329449984 | bytes 17825792 | tf_op jit(solution)/shard_map/frn,ncm->frcm/dot_general | solution.py:22
  151.7 19.1 %constant_dynamic-slice_fusion.6 = (bf16[48,256,128]{2,1,0:T(8,128)(2,1)}, bf16[48,256,128]{2,1,0:T(8,128)(2,1)}, bf16[48,256,128]{2,1,0:T(8,128)(2,1)}, bf16[48...) fusion(bf16[48,256,1024]{2,1,0:T(8,128)(2,1)} %param.7, ...), kind=kLoop, calls=%fused_computation.75 | loop fusion | bytes 50331680 | tf_op jit(solution)/shard_map/dynamic_slice | solution.py:61
  170.8 37.9 %reduce-scatter.2.cloned.1.call-done = f32[16,48,2,256]{3,1,2,0:T(8,128)} async-done(((f32[16,48,2,1024]{3,1,2,0:T(8,128)}), f32[16,48,2,256]{3,1,2,0:T(8,128)}) %reduce-scatter.2.cloned.1.call-update) | async-done | bytes 1572880 | tf_op jit(solution)/shard_map/reduce_scatter | solution.py:88
  208.7 1.5 convert_element_type.83
  210.2 3.2 copy.42
  213.4 4.0 convert_bitcast_fusion
  217.5 1.5 collective-permute-start.5
  219.0 2.0 convert_bitcast_fusion.2
  221.6 2.0 convert_bitcast_fusion.1
  223.6 1.5 collective-permute-start.3
  225.2 2.0 convert_bitcast_fusion.3
  227.8 38.2 %collective-permute-done.5 = bf16[128,16,2,256]{0,1,2,3:T(8,128)(2,1)S(1)} collective-permute-done((bf16[128,16,2,256]{0,1,2,3:T(8,128)(2,1)S(1)}, bf16[128,16,2,256]{0,1,2,3:T(8,128)(2,1)S(1)}, u32[]{:S(2)}, u32[]{:S(2)}) %collective-permute-start.5) | collective-permute-done | bytes 2097184 | tf_op jit(solution)/shard_map/ppermute | solution.py:67
  266.0 2.5 fusion.6
  268.5 3.6 collective-permute-start.6
  272.2 38.8 %collective-permute-done.1 = bf16[128,16,2,256]{0,1,2,3:T(8,128)(2,1)S(1)} collective-permute-done((bf16[128,16,2,256]{0,1,2,3:T(8,128)(2,1)S(1)}, bf16[128,16,2,256]{0,1,2,3:T(8,128)(2,1)S(1)}, u32[]{:S(2)}, u32[]{:S(2)}) %collective-permute-start.1) | collective-permute-done | bytes 2097184 | tf_op jit(solution)/shard_map/ppermute | solution.py:67
  311.0 2.5 fusion.8
  313.5 2.5 collective-permute-start.2
  315.9 40.0 %collective-permute-done.3 = bf16[128,16,2,256]{0,1,2,3:T(8,128)(2,1)S(1)} collective-permute-done((bf16[128,16,2,256]{0,1,2,3:T(8,128)(2,1)S(1)}, bf16[128,16,2,256]{0,1,2,3:T(8,128)(2,1)S(1)}, u32[]{:S(2)}, u32[]{:S(2)}) %collective-permute-start.3) | collective-permute-done | bytes 2097184 | tf_op jit(solution)/shard_map/ppermute | solution.py:67
  355.9 2.5 fusion.7
  358.4 1.5 collective-permute-start.4
  359.9 2.1 fusion.26
  362.0 37.6 %collective-permute-done = bf16[128,16,2,256]{0,1,2,3:T(8,128)(2,1)S(1)} collective-permute-done((bf16[128,16,2,256]{0,1,2,3:T(8,128)(2,1)S(1)}, bf16[128,16,2,256]{0,1,2,3:T(8,128)(2,1)S(1)}, u32[]{:S(2)}, u32[]{:S(2)}) %collective-permute-start) | collective-permute-done | bytes 2097184 | tf_op jit(solution)/shard_map/ppermute | solution.py:67
  399.6 50.1 %collective-permute-done.2 = bf16[128,16,2,256]{0,1,2,3:T(8,128)(2,1)S(1)} collective-permute-done((bf16[128,16,2,256]{0,1,2,3:T(8,128)(2,1)S(1)}, bf16[128,16,2,256]{0,1,2,3:T(8,128)(2,1)S(1)}, u32[]{:S(2)}, u32[]{:S(2)}) %collective-permute-start.2) | collective-permute-done | bytes 2097184 | tf_op jit(solution)/shard_map/ppermute | solution.py:74
  449.6 3.4 fusion.11
  453.0 5.8 %copy.57 = f32[128,16,2,256]{3,2,1,0:T(2,128)} copy(f32[128,16,2,256]{0,1,2,3:T(8,128)} %fusion.11) | data formatting | bytes 8388608 | tf_op jit(solution)/shard_map/add | solution.py:77
  (37 shorter events, 3.0 us)
Async XLA Ops:
  18.8 7.5 %copy-start.8 = (s32[512]{0:T(512)S(1)}, s32[512]{0:T(512)}, u32[]{:S(2)}) copy-start(s32[512]{0:T(512)} %param.6) | copy-start | bytes 6148
  18.8 100.7 %all-to-all-start = ((f32[16,64,1024]{2,0,1:T(8,128)}), f32[16,64,1024]{2,0,1:T(8,128)}, u32[]{:S(2)}, u32[]{:S(2)}) async-start(f32[16,64,1024]{2,0,1:T(8,128)} %copy.39), calls=%async_computation | async-start | bytes 8388608 | tf_op jit(solution)/shard_map/all_to_all | solution.py:41
  26.2 182.4 %reduce-scatter.2.cloned.1.call-start = ((), (), s32[]{:S(2)}) async-start(), calls=%async_computation.2 | async-start | bytes 7864320 | tf_op jit(solution)/shard_map/reduce_scatter | solution.py:88
  119.5 8.2 %copy-start.7 = (f32[1024,1,1024]{2,0,1:T(8,128)S(1)}, f32[1024,1,1024]{2,0,1:T(8,128)}, u32[]{:S(2)}) copy-start(f32[1024,1,1024]{2,0,1:T(8,128)} %get-tuple-element.18) | copy-start | bytes 12582916
  213.4 5.6 %copy-start.2 = (bf16[48,256,128]{2,1,0:T(8,128)(2,1)S(1)}, bf16[48,256,128]{2,1,0:T(8,128)(2,1)}, u32[]{:S(2)}) copy-start(bf16[48,256,128]{2,1,0:T(8,128)(2,1)} %get-tuple-element.12) | copy-start | bytes 9437188
  217.5 48.6 %collective-permute-start.5 = (bf16[128,16,2,256]{0,1,2,3:T(8,128)(2,1)S(1)}, bf16[128,16,2,256]{0,1,2,3:T(8,128)(2,1)S(1)}, u32[]{:S(2)}, u32[]{:S(2)}) collective-permute-start(bf16[128,16,2,256]{0,1,2,3:T(8,128)(2,1)S(1)} %convert_bitcast_fusion), channel_id=1, source_target_pairs={{0,4},{4,0},{8,12},{12,8},{16,20},{20,16},{24,28},{28,24},{1,5},{5... | collective-permute-start | bytes 6291464 | tf_op jit(solution)/shard_map/ppermute | solution.py:67
  219.0 2.6 copy-start.1
  221.0 90.0 %collective-permute-start.1 = (bf16[128,16,2,256]{0,1,2,3:T(8,128)(2,1)S(1)}, bf16[128,16,2,256]{0,1,2,3:T(8,128)(2,1)S(1)}, u32[]{:S(2)}, u32[]{:S(2)}) collective-permute-start(bf16[128,16,2,256]{0,1,2,3:T(8,128)(2,1)S(1)} %convert_bitcast_fusion.2), channel_id=1, source_target_pairs={{0,4},{4,0},{8,12},{12,8},{16,20},{20,16},{24,28},{28,24},{1,5},{5... | collective-permute-start | bytes 6291464 | tf_op jit(solution)/shard_map/ppermute | solution.py:67
  221.6 3.5 copy-start
  223.6 132.3 %collective-permute-start.3 = (bf16[128,16,2,256]{0,1,2,3:T(8,128)(2,1)S(1)}, bf16[128,16,2,256]{0,1,2,3:T(8,128)(2,1)S(1)}, u32[]{:S(2)}, u32[]{:S(2)}) collective-permute-start(bf16[128,16,2,256]{0,1,2,3:T(8,128)(2,1)S(1)} %convert_bitcast_fusion.1), channel_id=1, source_target_pairs={{0,4},{4,0},{8,12},{12,8},{16,20},{20,16},{24,28},{28,24},{1,5},{5... | collective-permute-start | bytes 6291464 | tf_op jit(solution)/shard_map/ppermute | solution.py:67
  225.2 40.9 %copy-start.6 = (bf16[48,256,128]{2,1,0:T(8,128)(2,1)S(1)}, bf16[48,256,128]{2,1,0:T(8,128)(2,1)}, u32[]{:S(2)}) copy-start(bf16[48,256,128]{2,1,0:T(8,128)(2,1)} %get-tuple-element.9) | copy-start | bytes 9437188
  227.2 172.4 %collective-permute-start = (bf16[128,16,2,256]{0,1,2,3:T(8,128)(2,1)S(1)}, bf16[128,16,2,256]{0,1,2,3:T(8,128)(2,1)S(1)}, u32[]{:S(2)}, u32[]{:S(2)}) collective-permute-start(bf16[128,16,2,256]{0,1,2,3:T(8,128)(2,1)S(1)} %convert_bitcast_fusion.3), channel_id=1, source_target_pairs={{0,4},{4,0},{8,12},{12,8},{16,20},{20,16},{24,28},{28,24},{1,5},{5... | collective-permute-start | bytes 6291464 | tf_op jit(solution)/shard_map/ppermute | solution.py:67
  266.0 44.9 %copy-start.5 = (bf16[48,256,128]{2,1,0:T(8,128)(2,1)S(1)}, bf16[48,256,128]{2,1,0:T(8,128)(2,1)}, u32[]{:S(2)}) copy-start(bf16[48,256,128]{2,1,0:T(8,128)(2,1)} %get-tuple-element.13) | copy-start | bytes 9437188
  268.5 131.0 %collective-permute-start.6 = (bf16[128,16,2,256]{0,1,2,3:T(8,128)(2,1)S(1)}, bf16[128,16,2,256]{0,1,2,3:T(8,128)(2,1)S(1)}, u32[]{:S(2)}, u32[]{:S(2)}) collective-permute-start(bf16[128,16,2,256]{0,1,2,3:T(8,128)(2,1)S(1)} %fusion.6), channel_id=1, source_target_pairs={{0,24},{4,28},{8,0},{12,4},{16,8},{20,12},{24,16},{28,20},{1,25},{... | collective-permute-start | bytes 6291464 | tf_op jit(solution)/shard_map/ppermute | solution.py:74
  311.0 44.9 %copy-start.4 = (bf16[48,256,128]{2,1,0:T(8,128)(2,1)S(1)}, bf16[48,256,128]{2,1,0:T(8,128)(2,1)}, u32[]{:S(2)}) copy-start(bf16[48,256,128]{2,1,0:T(8,128)(2,1)} %get-tuple-element.11) | copy-start | bytes 9437188
  313.5 136.2 %collective-permute-start.2 = (bf16[128,16,2,256]{0,1,2,3:T(8,128)(2,1)S(1)}, bf16[128,16,2,256]{0,1,2,3:T(8,128)(2,1)S(1)}, u32[]{:S(2)}, u32[]{:S(2)}) collective-permute-start(bf16[128,16,2,256]{0,1,2,3:T(8,128)(2,1)S(1)} %fusion.8), channel_id=1, source_target_pairs={{0,16},{4,20},{8,24},{12,28},{16,0},{20,4},{24,8},{28,12},{1,17},{... | collective-permute-start | bytes 6291464 | tf_op jit(solution)/shard_map/ppermute | solution.py:74
  355.9 4.0 copy-start.3
  358.4 91.2 %collective-permute-start.4 = (bf16[128,16,2,256]{0,1,2,3:T(8,128)(2,1)S(1)}, bf16[128,16,2,256]{0,1,2,3:T(8,128)(2,1)S(1)}, u32[]{:S(2)}, u32[]{:S(2)}) collective-permute-start(bf16[128,16,2,256]{0,1,2,3:T(8,128)(2,1)S(1)} %fusion.7), channel_id=1, source_target_pairs={{0,8},{4,12},{8,16},{12,20},{16,24},{20,28},{24,0},{28,4},{1,9},{5... | collective-permute-start | bytes 6291464 | tf_op jit(solution)/shard_map/ppermute | solution.py:74
Sparse Core Ops, SparseCore 0:
  151.7 56.9 reduce-scatter.1
